TPU v7x, 256 devices: a whole 4x4x8 slice. The times are simulated.
256 devices in a mesh: side: 2 (over core), group: 16 (over y, z_lo), head: 8 (over x, z_hi).
Axes of the slice: x: 4, y: 4, z: 8 (z_hi: 2, z_lo: 4; z = z_hi * 4 + z_lo), core: 2. Of those that a mesh axis runs over, the one named last changes fastest.
Arguments:
- pool_rows: bfloat16 [2, 6144, 4096], P('side', ('group', 'head')), may hold values from -24 to 24
- pool_weight: bfloat16 [2, 4096, 8192], P('side', 'group', 'head'), as said below
- lengths: int32 [16, 3], replicated, may hold values from 1 to 192, 384 in all within a row
- owner: int32 [16, 3], replicated, may hold values from 0 to 15, as said below
Outputs:
- pool_out: bfloat16 [2, 6144, 4096], P('side', 'group', 'head')
Inputs may be any that keep to these rules, and one draw needn't show every extreme that they name: owner[p, j] is p with the binary digits of m_j flipped, where m_j = owner[0, j] is the same for every p; the m_j differ between slots, and every binary digit below 16 is set in some m_j. So the 3 requests of a prefill group go to different decode groups, and every decode group receives exactly one request for each slot j. `lengths`: each row sums to 384. `pool_weight`: independent normal entries of deviation 1 / sqrt(4096).
All inputs are finite; a program needn't handle non-finite values.
Results may differ from a plain program's by a relative error of at most 0.0061.
Values may be sent and summed in bfloat16 or wider, within the bound.
No kernel may reach another device: no remote copies, remote signals or barrier semaphores. Data moves between devices by JAX's collectives and lax.ppermute only.
A program may use at most 128 MiB of HBM per device.

v0:
```python
import jax
import jax.numpy as jnp
from jax import lax
from jax.sharding import Mesh
from jax.sharding import PartitionSpec as P

HEAD_DIM = 256
GROUP = ("group_0", "group_1")
GROUP_HEAD = ("group_0", "group_1", "head")


def whole_of(value, axes, dim):
    for axis in reversed(axes):
        value = lax.all_gather(value, axis, axis=dim, tiled=True)
    return value


def shifted(value, axis, by):
    count = lax.axis_size(axis)
    pairs = [(i, i + by) for i in range(count) if 0 <= i + by < count]
    return lax.ppermute(value, axis, pairs)


def swapped(block, axis, bit):
    count = lax.axis_size(axis)
    route = []
    for low in range(count):
        high = low | 1 << bit
        if high != low and high < count:
            route += [(low, high), (high, low)]
    return lax.ppermute(block, axis, route)


def attend_direct(query_rows, memory_rows, count, wide, scale):
    maxlen = memory_rows.shape[0]
    rows = query_rows.shape[0]
    heads_dev = wide // HEAD_DIM
    queries = query_rows.reshape(rows, heads_dev, HEAD_DIM)
    key_rows = memory_rows[:, :wide].reshape(maxlen, heads_dev, HEAD_DIM)
    value_rows = memory_rows[:, wide:].reshape(maxlen, heads_dev, HEAD_DIM)
    scores = (
        jnp.einsum("qeh,keh->eqk", queries, key_rows, preferred_element_type=jnp.float32) * scale
    )
    valid = jnp.arange(maxlen, dtype=jnp.int32) < count
    scores = jnp.where(valid[None, None, :], scores, -1e30)
    peak = jnp.max(scores, axis=-1, keepdims=True)
    expo = jnp.where(valid[None, None, :], jnp.exp(scores - peak), 0.0)
    total = jnp.sum(expo, axis=-1)
    mixed = jnp.einsum(
        "eqk,keh->eqh", expo.astype(jnp.bfloat16), value_rows, preferred_element_type=jnp.float32
    )
    mixed = mixed / total[:, :, None]
    return jnp.transpose(mixed, (1, 0, 2)).reshape(rows, wide)


def on_device(pool_rows, pool_weight, lengths, owner):
    side_index = lax.axis_index("side")
    group_index = lax.axis_index(GROUP)
    requests = lengths.shape[1]
    gathered = lax.all_gather(pool_rows[0], "head", axis=0, tiled=True)
    weight = whole_of(pool_weight[0], GROUP, 0)
    mem_g = gathered.shape[0]
    wide = weight.shape[1] // 2
    q_req = mem_g // requests
    maxlen = mem_g // 2
    scale = 1.0 / HEAD_DIM**0.5
    cached = jnp.dot(gathered, weight, preferred_element_type=jnp.float32).astype(jnp.bfloat16)
    queries = cached[:, :wide]
    starts = jnp.cumsum(lengths, axis=1) - lengths
    groups = jnp.arange(lengths.shape[0], dtype=jnp.int32)
    sources, begins, counts = ([], [], [])
    for slot in range(requests):
        hit = owner[:, slot] == group_index
        sources.append(jnp.sum(jnp.where(hit, groups, 0)))
        begins.append(jnp.sum(jnp.where(hit, starts[:, slot], 0)))
        counts.append(jnp.sum(jnp.where(hit, lengths[:, slot], 0)))
    moved = shifted(cached, "side", 1)
    padded = jnp.concatenate([moved, jnp.zeros((maxlen, moved.shape[1]), jnp.bfloat16)], axis=0)
    own_starts = lax.dynamic_index_in_dim(starts, group_index, 0, keepdims=False)
    holding = jnp.stack(
        [lax.dynamic_slice_in_dim(padded, own_starts[slot], maxlen, 0) for slot in range(requests)],
        axis=0,
    )
    flips = owner[0]
    for digit in range(lax.axis_size(GROUP).bit_length() - 1):
        partner = swapped(holding, GROUP, digit)
        moving = jnp.bitwise_and(jnp.right_shift(flips, digit), 1) == 1
        holding = jnp.where(moving[:, None, None], partner, holding)
    pieces = []
    for slot in range(requests):
        query_rows = queries[slot * q_req : (slot + 1) * q_req]
        pieces.append(attend_direct(query_rows, holding[slot], counts[slot], wide, scale))
    attended = jnp.concatenate(pieces, axis=0).astype(jnp.bfloat16)
    partial_out = lax.dot_general(
        attended, weight[:, wide:], (((1,), (1,)), ((), ())), preferred_element_type=jnp.float32
    )
    decoded = lax.psum_scatter(partial_out, "head", scatter_dimension=1, tiled=True).astype(
        jnp.bfloat16
    )
    result = jnp.where(side_index == 0, cached[:, :wide], decoded)
    return result[None]


def solution(mesh):
    torus = Mesh(
        mesh.devices.reshape(mesh.shape["side"], 4, 4, mesh.shape["head"]),
        ("side", "group_0", "group_1", "head"),
    )
    in_specs = (P("side", GROUP_HEAD, None), P("side", GROUP, "head"), P(), P())
    out_specs = P("side", GROUP, "head")
    return jax.shard_map(
        on_device, mesh=torus, in_specs=in_specs, out_specs=out_specs, check_vma=False
    )
```

profile of v0, /device:TPU:8, one launch (start us, length us, event | category | flops | bytes accessed | tf_op | source)
XLA Modules:
  0.0 563.7 jit_solution(15055022247647864078)
XLA Ops:
  6.5 0.0 all-gather.9.cloned.1.call-start
  6.5 0.7 all-gather.9.cloned.1.call-update
  7.3 0.0 all-gather.7.cloned.1.call-start
  7.3 0.7 all-gather.7.cloned.1.call-update
  8.0 0.0 all-gather.11.cloned.1.call-start
  8.1 54.0 %all-gather.9.cloned.1.call-done = bf16[1,1024,1024]{2,1,0:T(8,128)(2,1)} async-done(((bf16[1,256,1024]{2,1,0:T(8,128)(2,1)}), bf16[1,1024,1024]{2,1,0:T(8,128)(2,1)}) %all-gather.9.cloned.1.call-update) | async-done | bytes 2097168 | tf_op jit(solution)/shard_map/all_gather | solution.py:14
  62.0 0.0 all-gather.11.cloned.1.call-update
  62.0 0.0 copy-start
  62.1 0.0 reduce-scatter.2.cloned.1.call-start
  62.1 93.6 %all-gather.7.cloned.1.call-done = bf16[1,384,4096]{2,1,0:T(8,128)(2,1)} async-done(((bf16[1,48,4096]{2,1,0:T(8,128)(2,1)}), bf16[1,384,4096]{2,1,0:T(8,128)(2,1)}) %all-gather.7.cloned.1.call-update) | async-done | bytes 3145744 | tf_op jit(solution)/shard_map/all_gather | solution.py:60
  155.7 82.9 %all-gather.11.cloned.1.call-done = bf16[1,4096,1024]{2,1,0:T(8,128)(2,1)} async-done(((bf16[1,1024,1024]{2,1,0:T(8,128)(2,1)}), bf16[1,4096,1024]{2,1,0:T(8,128)(2,1)}) %all-gather.11.cloned.1.call-update) | async-done | bytes 8388624 | tf_op jit(solution)/shard_map/all_gather | solution.py:14
  238.6 7.7 %fusion.7 = bf16[384,1024]{1,0:T(8,128)(2,1)S(1)} fusion(bf16[1,384,4096]{2,1,0:T(8,128)(2,1)} %all-gather.7.cloned.1.call-done, bf16[1,4096,1024]{2,1,0:T(8,128)(2,1)} %all-gather.11.cloned.1.call-done), kind=kOutput, calls=%fused_computation.7 | convolution fusion | flops 3221618688 | bytes 12320768 | tf_op jit(solution)/shard_map/dot_general | solution.py:67
  246.4 1.6 collective-permute-start
  248.0 0.0 copy-done
  248.1 0.1 constant_dynamic-slice_fusion
  248.1 0.5 fusion.77
  254.2 0.0 collective-permute-done
  254.2 0.8 fusion.28
  255.0 0.0 copy-start.1
  255.0 0.1 pad_maximum_fusion
  255.2 1.6 collective-permute-start.1
  256.8 0.0 copy-done.1
  256.8 0.1 fusion.58
  256.9 25.5 %collective-permute-done.1 = bf16[3,192,1024]{2,1,0:T(8,128)(2,1)S(1)} collective-permute-done((bf16[3,192,1024]{2,1,0:T(8,128)(2,1)S(1)}, bf16[3,192,1024]{2,1,0:T(8,128)(2,1)S(1)}, u32[]{:S(2)}, u32[]{:S(2)}) %collective-permute-start.1) | collective-permute-done | bytes 1179680 | tf_op jit(solution)/shard_map/ppermute | solution.py:31
  282.5 0.2 broadcast_select_fusion
  282.7 2.6 collective-permute-start.2
  285.3 50.0 %collective-permute-done.2 = bf16[3,192,1024]{2,1,0:T(8,128)(2,1)S(1)} collective-permute-done((bf16[3,192,1024]{2,1,0:T(8,128)(2,1)S(1)}, bf16[3,192,1024]{2,1,0:T(8,128)(2,1)S(1)}, u32[]{:S(2)}, u32[]{:S(2)}) %collective-permute-start.2) | collective-permute-done | bytes 1179680 | tf_op jit(solution)/shard_map/ppermute | solution.py:31
  335.3 0.3 broadcast_select_fusion.1
  335.5 0.7 collective-permute-start.3
  336.2 26.3 %collective-permute-done.3 = bf16[3,192,1024]{2,1,0:T(8,128)(2,1)S(1)} collective-permute-done((bf16[3,192,1024]{2,1,0:T(8,128)(2,1)S(1)}, bf16[3,192,1024]{2,1,0:T(8,128)(2,1)S(1)}, u32[]{:S(2)}, u32[]{:S(2)}) %collective-permute-start.3) | collective-permute-done | bytes 1179680 | tf_op jit(solution)/shard_map/ppermute | solution.py:31
  362.5 0.2 broadcast_select_fusion.2
  362.7 1.4 collective-permute-start.4
  364.1 0.7 fusion.65
  364.8 0.6 iota_compare_fusion.2
  365.5 1.2 iota_compare_fusion
  366.7 23.7 %collective-permute-done.4 = bf16[3,192,1024]{2,1,0:T(8,128)(2,1)S(1)} collective-permute-done((bf16[3,192,1024]{2,1,0:T(8,128)(2,1)S(1)}, bf16[3,192,1024]{2,1,0:T(8,128)(2,1)S(1)}, u32[]{:S(2)}, u32[]{:S(2)}) %collective-permute-start.4) | collective-permute-done | bytes 1179680 | tf_op jit(solution)/shard_map/ppermute | solution.py:31
  390.4 0.2 broadcast_select_fusion.3
  390.5 0.1 slice_bitcast_fusion.2
  390.6 0.1 fusion.74
  390.7 0.2 fusion.21
  390.9 0.1 fusion.80
  391.0 0.3 fusion.16
  391.3 0.1 copy.11
  391.5 0.2 fusion.20
  391.7 0.1 fusion.79
  391.8 0.3 fusion.17
  392.1 0.1 copy.15
  392.3 0.2 fusion.19
  392.5 0.1 fusion.78
  392.6 0.3 fusion.18
  392.9 0.1 copy.19
  393.0 6.8 %fusion.3 = f32[384,4096]{1,0:T(8,128)} fusion(bf16[4096,1024]{1,0:T(8,128)(2,1)} %bitcast.91, bf16[128,512]{0,1:T(8,128)(2,1)S(1)} %bitcast.94, bf16[128,512]{0,1:T(8,128)(2,1)S(1)} %bitcast.93, bf16[128,512]{0,1:T(8,128)(2,1)S(1)} %bitcast.92), kind=kOutput, calls=%fused_computation.3 | convolution fusion | flops 1611792384 | bytes 10878976 | tf_op jit(solution)/shard_map/dot_general | solution.py:94
  399.8 0.0 reduce-scatter.2.cloned.1.call-update
  399.9 155.4 %reduce-scatter.2.cloned.1.call-done = f32[384,512]{1,0:T(8,128)} async-done(((f32[384,4096]{1,0:T(8,128)}), f32[384,512]{1,0:T(8,128)}) %reduce-scatter.2.cloned.1.call-update) | async-done | bytes 786448 | tf_op jit(solution)/shard_map/reduce_scatter | solution.py:97
  555.3 1.9 fusion.31
  (4 shorter events, 0.1 us)
Async XLA Ops:
  6.5 55.5 %all-gather.9.cloned.1.call-start = ((), (), s32[]{:S(2)}) async-start(), calls=%async_computation.3 | async-start | bytes 2621440 | tf_op jit(solution)/shard_map/all_gather | solution.py:14
  7.3 148.5 %all-gather.7.cloned.1.call-start = ((), (), s32[]{:S(2)}) async-start(), calls=%async_computation.2 | async-start | bytes 3538944 | tf_op jit(solution)/shard_map/all_gather | solution.py:60
  8.0 230.6 %all-gather.11.cloned.1.call-start = ((), (), s32[]{:S(2)}) async-start(), calls=%async_computation.4 | async-start | bytes 10485760 | tf_op jit(solution)/shard_map/all_gather | solution.py:14
  62.0 186.0 %copy-start = (s32[16,3]{0,1:T(4,128)S(1)}, s32[16,3]{0,1:T(4,128)}, u32[]{:S(2)}) copy-start(s32[16,3]{0,1:T(4,128)} %param.6) | copy-start | bytes 580
  62.1 493.2 %reduce-scatter.2.cloned.1.call-start = ((), (), s32[]{:S(2)}) async-start(), calls=%async_computation.1 | async-start | bytes 7077888 | tf_op jit(solution)/shard_map/reduce_scatter | solution.py:97
  246.4 7.8 %collective-permute-start = (bf16[384,1024]{1,0:T(8,128)(2,1)S(1)}, bf16[384,1024]{1,0:T(8,128)(2,1)S(1)}, u32[]{:S(2)}, u32[]{:S(2)}) collective-permute-start(bf16[384,1024]{1,0:T(8,128)(2,1)S(1)} %fusion.7), channel_id=1, source_target_pairs={{0,128},{1,129},{2,130},{3,131},{4,132},{5,133},{6,134},{7,135},{8... | collective-permute-start | bytes 2359304 | tf_op jit(solution)/shard_map/ppermute | solution.py:21
  255.0 1.8 copy-start.1
  255.2 27.3 %collective-permute-start.1 = (bf16[3,192,1024]{2,1,0:T(8,128)(2,1)S(1)}, bf16[3,192,1024]{2,1,0:T(8,128)(2,1)S(1)}, u32[]{:S(2)}, u32[]{:S(2)}) collective-permute-start(bf16[3,192,1024]{2,1,0:T(8,128)(2,1)S(1)} %pad_maximum_fusion), channel_id=1, source_target_pairs={{0,8},{8,0},{16,24},{24,16},{32,40},{40,32},{48,56},{56,48},{64,72... | collective-permute-start | bytes 3538952 | tf_op jit(solution)/shard_map/ppermute | solution.py:31
  282.7 52.6 %collective-permute-start.2 = (bf16[3,192,1024]{2,1,0:T(8,128)(2,1)S(1)}, bf16[3,192,1024]{2,1,0:T(8,128)(2,1)S(1)}, u32[]{:S(2)}, u32[]{:S(2)}) collective-permute-start(bf16[3,192,1024]{2,1,0:T(8,128)(2,1)S(1)} %broadcast_select_fusion), channel_id=1, source_target_pairs={{0,16},{16,0},{8,24},{24,8},{32,48},{48,32},{40,56},{56,40},{64,80... | collective-permute-start | bytes 3538952 | tf_op jit(solution)/shard_map/ppermute | solution.py:31
  335.5 27.0 %collective-permute-start.3 = (bf16[3,192,1024]{2,1,0:T(8,128)(2,1)S(1)}, bf16[3,192,1024]{2,1,0:T(8,128)(2,1)S(1)}, u32[]{:S(2)}, u32[]{:S(2)}) collective-permute-start(bf16[3,192,1024]{2,1,0:T(8,128)(2,1)S(1)} %broadcast_select_fusion.1), channel_id=1, source_target_pairs={{0,32},{32,0},{8,40},{40,8},{16,48},{48,16},{24,56},{56,24},{64,96... | collective-permute-start | bytes 3538952 | tf_op jit(solution)/shard_map/ppermute | solution.py:31
  362.7 27.6 %collective-permute-start.4 = (bf16[3,192,1024]{2,1,0:T(8,128)(2,1)S(1)}, bf16[3,192,1024]{2,1,0:T(8,128)(2,1)S(1)}, u32[]{:S(2)}, u32[]{:S(2)}) collective-permute-start(bf16[3,192,1024]{2,1,0:T(8,128)(2,1)S(1)} %broadcast_select_fusion.2), channel_id=1, source_target_pairs={{0,64},{64,0},{8,72},{72,8},{16,80},{80,16},{24,88},{88,24},{32,96... | collective-permute-start | bytes 3538952 | tf_op jit(solution)/shard_map/ppermute | solution.py:31
Sparse Core Ops, SparseCore 0:
  9.1 52.8 all-gather.8
  64.6 91.0 all-gather.6
  157.5 81.0 all-gather.10
  400.0 155.2 reduce-scatter.1
where the time goes:
time: 564 us
  waiting for transfers between devices  513 us (91%)
  between operations  18.8 us (3%)
  matrix products  16.1 us (3%)
  starting transfers between devices  8.07 us (1%)
  other arithmetic  5.96 us (1%)
    reduce_scatter x1, waiting for transfers between devices, on_device(): lax.psum_scatter(partial_out, 'head', scatter_dimension=1, tiled=True)  155 us
    all_gather x2, waiting for transfers between devices, whole_of(): value = lax.all_gather(value, axis, axis=dim, tiled=True)  137 us
    ppermute x4, waiting for transfers between devices, swapped(): return lax.ppermute(block, axis, route)  125 us
    all_gather x1, waiting for transfers between devices, on_device(): gathered = lax.all_gather(pool_rows[0], 'head', axis=0, tiled=True)  93.6 us
  transfers between devices with their start and end apart: 9, of which 8 were waited for; matrix products, arithmetic and copies ran while one was open for 1% of the time, Pallas kernels for 0%

commit v1 on v0

--- a/solution.py
+++ b/solution.py
@@ -57,7 +57,9 @@
     side_index = lax.axis_index("side")
     group_index = lax.axis_index(GROUP)
     requests = lengths.shape[1]
-    gathered = lax.all_gather(pool_rows[0], "head", axis=0, tiled=True)
+    gathered = jnp.concatenate(
+        lax.all_to_all(jnp.stack([pool_rows[0]] * lax.axis_size("head")), "head", 0, 0), axis=0
+    )
     weight = whole_of(pool_weight[0], GROUP, 0)
     mem_g = gathered.shape[0]
     wide = weight.shape[1] // 2

time: 564 us -> 474 us (0.84)
  waiting for transfers between devices: 513 us -> 340 us
  blocking collectives: 0 us -> 82.3 us
    all_gather x1 -> x0, waiting for transfers between devices: 93.6 us -> none  [on_device(): gathered = lax.all_gather(pool_rows[0], 'head', axis=0, tiled=True)]
    all_to_all x0 -> x1, blocking collectives: none -> 82.3 us  [on_device(): lax.all_to_all(jnp.stack([pool_rows[0]] * lax.axis_size('head')), 'head',...]
    all_gather x2, waiting for transfers between devices: 137 us -> 59.1 us  [whole_of(): value = lax.all_gather(value, axis, axis=dim, tiled=True)]
  transfers between devices with their start and end apart: 9 -> 8, of which waited for: 8 -> 7; matrix products, arithmetic and copies ran while one was open for 1% -> 1% of each run, Pallas kernels for 0% -> 0%
where the time goes in v1:
time: 474 us; the launch traced here: 473 us
  waiting for transfers between devices  340 us (72%)
  blocking collectives  82.3 us (17%)
  between operations  18.8 us (4%)
  matrix products  15.1 us (3%)
  starting transfers between devices  8.01 us (2%)
  other arithmetic  6.08 us (1%)
    reduce_scatter x1, waiting for transfers between devices, on_device(): lax.psum_scatter(partial_out, 'head', scatter_dimension=1, tiled=True)  155 us
    ppermute x4, waiting for transfers between devices, swapped(): return lax.ppermute(block, axis, route)  124 us
    all_to_all x1, blocking collectives, on_device(): lax.all_to_all(jnp.stack([pool_rows[0]] * lax.axis_size('head')), 'head',...  82.3 us
    all_gather x2, waiting for transfers between devices, whole_of(): value = lax.all_gather(value, axis, axis=dim, tiled=True)  59.1 us
  transfers between devices with their start and end apart: 8, of which 7 were waited for; matrix products, arithmetic and copies ran while one was open for 1% of the time, Pallas kernels for 0%

profile of v1, /device:TPU:8, one launch (start us, length us, event | category | flops | bytes accessed | tf_op | source)
XLA Modules:
  0.0 473.4 jit_solution(6060865188185372267)
XLA Ops:
  6.5 0.0 all-gather.5.cloned.1.call-start
  6.5 0.7 all-gather.5.cloned.1.call-update
  7.3 0.0 copy-start
  7.3 0.0 all-gather.7.cloned.1.call-start
  7.3 54.7 %all-gather.5.cloned.1.call-done = bf16[1,1024,1024]{2,1,0:T(8,128)(2,1)} async-done(((bf16[1,256,1024]{2,1,0:T(8,128)(2,1)}), bf16[1,1024,1024]{2,1,0:T(8,128)(2,1)}) %all-gather.5.cloned.1.call-update) | async-done | bytes 2097168 | tf_op jit(solution)/shard_map/all_gather | solution.py:14
  62.0 0.0 all-gather.7.cloned.1.call-update
  62.0 0.0 reduce-scatter.2.cloned.1.call-start
  62.1 0.0 copy-done
  62.1 0.4 stack.15
  62.5 82.3 %all_to_all.5 = bf16[8,48,4096]{2,1,0:T(8,128)(2,1)S(1)} all-to-all(bf16[8,48,4096]{2,1,0:T(8,128)(2,1)S(1)} %stack.15), channel_id=1, replica_groups=mesh['side'=2,'group_0'=4,'group_1'=4,'head'=8] {'head'}, dimensions={0} | all-to-all | bytes 6291456 | tf_op jit(solution)/shard_map/all_to_all | solution.py:61
  144.7 4.3 all-gather.7.cloned.1.call-done
  149.1 0.0 copy-start.1
  149.1 6.8 %convolution_convert_fusion = bf16[384,1024]{1,0:T(8,128)(2,1)} fusion(bf16[384,4096]{1,0:T(8,128)(2,1)S(1)} %bitcast.89, bf16[1,4096,1024]{2,1,0:T(8,128)(2,1)} %all-gather.7.cloned.1.call-done), kind=kOutput, calls=%fused_computation.5 | convolution fusion | flops 3221618688 | bytes 12320768 | tf_op jit(solution)/shard_map/dot_general | solution.py:69
  155.9 1.6 collective-permute-start
  157.5 0.0 copy-done.1
  157.5 0.1 constant_dynamic-slice_fusion
  157.6 0.5 fusion.72
  163.7 0.0 collective-permute-done
  163.7 0.8 fusion.23
  164.5 0.0 copy-start.2
  164.5 0.1 pad_maximum_fusion
  164.6 1.6 collective-permute-start.1
  166.3 0.0 copy-done.2
  166.3 0.1 fusion.53
  166.4 25.5 %collective-permute-done.1 = bf16[3,192,1024]{2,1,0:T(8,128)(2,1)S(1)} collective-permute-done((bf16[3,192,1024]{2,1,0:T(8,128)(2,1)S(1)}, bf16[3,192,1024]{2,1,0:T(8,128)(2,1)S(1)}, u32[]{:S(2)}, u32[]{:S(2)}) %collective-permute-start.1) | collective-permute-done | bytes 1179680 | tf_op jit(solution)/shard_map/ppermute | solution.py:31
  191.9 0.2 broadcast_select_fusion
  192.2 2.6 collective-permute-start.2
  194.8 50.0 %collective-permute-done.2 = bf16[3,192,1024]{2,1,0:T(8,128)(2,1)S(1)} collective-permute-done((bf16[3,192,1024]{2,1,0:T(8,128)(2,1)S(1)}, bf16[3,192,1024]{2,1,0:T(8,128)(2,1)S(1)}, u32[]{:S(2)}, u32[]{:S(2)}) %collective-permute-start.2) | collective-permute-done | bytes 1179680 | tf_op jit(solution)/shard_map/ppermute | solution.py:31
  244.8 0.3 broadcast_select_fusion.1
  245.0 0.7 collective-permute-start.3
  245.7 26.3 %collective-permute-done.3 = bf16[3,192,1024]{2,1,0:T(8,128)(2,1)S(1)} collective-permute-done((bf16[3,192,1024]{2,1,0:T(8,128)(2,1)S(1)}, bf16[3,192,1024]{2,1,0:T(8,128)(2,1)S(1)}, u32[]{:S(2)}, u32[]{:S(2)}) %collective-permute-start.3) | collective-permute-done | bytes 1179680 | tf_op jit(solution)/shard_map/ppermute | solution.py:31
  272.0 0.2 broadcast_select_fusion.2
  272.2 1.4 collective-permute-start.4
  273.6 0.7 fusion.60
  274.3 0.6 iota_compare_fusion.2
  274.9 1.2 iota_compare_fusion
  276.1 1.1 fusion.68
  277.2 22.6 %collective-permute-done.4 = bf16[3,192,1024]{2,1,0:T(8,128)(2,1)S(1)} collective-permute-done((bf16[3,192,1024]{2,1,0:T(8,128)(2,1)S(1)}, bf16[3,192,1024]{2,1,0:T(8,128)(2,1)S(1)}, u32[]{:S(2)}, u32[]{:S(2)}) %collective-permute-start.4) | collective-permute-done | bytes 1179680 | tf_op jit(solution)/shard_map/ppermute | solution.py:31
  299.8 0.2 broadcast_select_fusion.3
  300.0 0.1 slice_bitcast_fusion.2
  300.1 0.1 fusion.69
  300.2 0.2 fusion.16
  300.4 0.1 fusion.75
  300.5 0.3 fusion.11
  300.8 0.1 copy.11
  301.0 0.2 fusion.15
  301.2 0.1 fusion.74
  301.3 0.3 fusion.12
  301.6 0.1 copy.15
  301.7 0.2 fusion.14
  302.0 0.1 fusion.73
  302.1 0.3 fusion.13
  302.4 0.1 copy.19
  302.5 6.8 %fusion.3 = f32[384,4096]{1,0:T(8,128)} fusion(bf16[4096,1024]{1,0:T(8,128)(2,1)} %bitcast.90, bf16[128,512]{0,1:T(8,128)(2,1)S(1)} %bitcast.93, bf16[128,512]{0,1:T(8,128)(2,1)S(1)} %bitcast.92, bf16[128,512]{0,1:T(8,128)(2,1)S(1)} %bitcast.91), kind=kOutput, calls=%fused_computation.3 | convolution fusion | flops 1611792384 | bytes 10878976 | tf_op jit(solution)/shard_map/dot_general | solution.py:96
  309.3 0.0 reduce-scatter.2.cloned.1.call-update
  309.3 155.5 %reduce-scatter.2.cloned.1.call-done = f32[384,512]{1,0:T(8,128)} async-done(((f32[384,4096]{1,0:T(8,128)}), f32[384,512]{1,0:T(8,128)}) %reduce-scatter.2.cloned.1.call-update) | async-done | bytes 786448 | tf_op jit(solution)/shard_map/reduce_scatter | solution.py:99
  464.8 2.1 fusion.26
  (3 shorter events, 0.1 us)
Async XLA Ops:
  6.5 55.5 %all-gather.5.cloned.1.call-start = ((), (), s32[]{:S(2)}) async-start(), calls=%async_computation.3 | async-start | bytes 2621440 | tf_op jit(solution)/shard_map/all_gather | solution.py:14
  7.3 54.8 %copy-start = (bf16[1,48,4096]{2,1,0:T(8,128)(2,1)S(1)}, bf16[1,48,4096]{2,1,0:T(8,128)(2,1)}, u32[]{:S(2)}) copy-start(bf16[1,48,4096]{2,1,0:T(8,128)(2,1)} %param.4) | copy-start | bytes 1179652
  7.3 141.8 %all-gather.7.cloned.1.call-start = ((), (), s32[]{:S(2)}) async-start(), calls=%async_computation.4 | async-start | bytes 10485760 | tf_op jit(solution)/shard_map/all_gather | solution.py:14
  62.0 402.7 %reduce-scatter.2.cloned.1.call-start = ((), (), s32[]{:S(2)}) async-start(), calls=%async_computation.2 | async-start | bytes 7077888 | tf_op jit(solution)/shard_map/reduce_scatter | solution.py:99
  149.1 8.4 %copy-start.1 = (s32[16,3]{0,1:T(4,128)S(1)}, s32[16,3]{0,1:T(4,128)}, u32[]{:S(2)}) copy-start(s32[16,3]{0,1:T(4,128)} %param.6) | copy-start | bytes 580
  155.9 7.8 %collective-permute-start = (bf16[384,1024]{1,0:T(8,128)(2,1)}, bf16[384,1024]{1,0:T(8,128)(2,1)S(1)}, u32[]{:S(2)}, u32[]{:S(2)}) collective-permute-start(bf16[384,1024]{1,0:T(8,128)(2,1)} %convolution_convert_fusion), channel_id=1, source_target_pairs={{0,128},{1,129},{2,130},{3,131},{4,132},{5,133},{6,134},{7,135},{8... | collective-permute-start | bytes 2359304 | tf_op jit(solution)/shard_map/ppermute | solution.py:21
  164.5 1.8 copy-start.2
  164.6 27.3 %collective-permute-start.1 = (bf16[3,192,1024]{2,1,0:T(8,128)(2,1)S(1)}, bf16[3,192,1024]{2,1,0:T(8,128)(2,1)S(1)}, u32[]{:S(2)}, u32[]{:S(2)}) collective-permute-start(bf16[3,192,1024]{2,1,0:T(8,128)(2,1)S(1)} %pad_maximum_fusion), channel_id=1, source_target_pairs={{0,8},{8,0},{16,24},{24,16},{32,40},{40,32},{48,56},{56,48},{64,72... | collective-permute-start | bytes 3538952 | tf_op jit(solution)/shard_map/ppermute | solution.py:31
  192.2 52.6 %collective-permute-start.2 = (bf16[3,192,1024]{2,1,0:T(8,128)(2,1)S(1)}, bf16[3,192,1024]{2,1,0:T(8,128)(2,1)S(1)}, u32[]{:S(2)}, u32[]{:S(2)}) collective-permute-start(bf16[3,192,1024]{2,1,0:T(8,128)(2,1)S(1)} %broadcast_select_fusion), channel_id=1, source_target_pairs={{0,16},{16,0},{8,24},{24,8},{32,48},{48,32},{40,56},{56,40},{64,80... | collective-permute-start | bytes 3538952 | tf_op jit(solution)/shard_map/ppermute | solution.py:31
  245.0 27.0 %collective-permute-start.3 = (bf16[3,192,1024]{2,1,0:T(8,128)(2,1)S(1)}, bf16[3,192,1024]{2,1,0:T(8,128)(2,1)S(1)}, u32[]{:S(2)}, u32[]{:S(2)}) collective-permute-start(bf16[3,192,1024]{2,1,0:T(8,128)(2,1)S(1)} %broadcast_select_fusion.1), channel_id=1, source_target_pairs={{0,32},{32,0},{8,40},{40,8},{16,48},{48,16},{24,56},{56,24},{64,96... | collective-permute-start | bytes 3538952 | tf_op jit(solution)/shard_map/ppermute | solution.py:31
  272.2 27.6 %collective-permute-start.4 = (bf16[3,192,1024]{2,1,0:T(8,128)(2,1)S(1)}, bf16[3,192,1024]{2,1,0:T(8,128)(2,1)S(1)}, u32[]{:S(2)}, u32[]{:S(2)}) collective-permute-start(bf16[3,192,1024]{2,1,0:T(8,128)(2,1)S(1)} %broadcast_select_fusion.2), channel_id=1, source_target_pairs={{0,64},{64,0},{8,72},{72,8},{16,80},{80,16},{24,88},{88,24},{32,96... | collective-permute-start | bytes 3538952 | tf_op jit(solution)/shard_map/ppermute | solution.py:31
Sparse Core Ops, SparseCore 0:
  9.1 52.8 all-gather.4
  63.8 85.1 all-gather.6
  309.4 155.3 reduce-scatter.1
